TPU v7x, 32 devices: a whole 2x2x4 slice. The times are simulated.
32 devices in a mesh: curve: 4 (over y, core), group: 8 (over z, x).
Axes of the slice: x: 2, y: 2, z: 4, core: 2. Of those that a mesh axis runs over, the one named last changes fastest.
Arguments:
- right_side: float32 [125, 16384], P(None, ('curve', 'group')), may hold values from -6 to 6, as said below
- conductivity: float32 [16384], P(('curve', 'group')), may hold values from 0.3 to 3
- destination: int32 [16384], P(('curve', 'group')), may hold values from 0 to 16383, as said below
- neighbour: int32 [6, 16384], P(None, ('curve', 'group')), may hold values from -1 to 1023, as said below
- orientation: int32 [6, 16384], P(None, ('curve', 'group')), may hold values from 0 to 3, as said below
- send_list: int32 [2, 8192], P(None, ('curve', 'group')), may hold values from 0 to 511, as said below
Outputs:
- solution: float32 [125, 16384], P(None, ('curve', 'group'))
- residual: float32 [125, 16384], P(None, ('curve', 'group'))
Inputs may be any that keep to these rules, and one draw needn't show every extreme that they name: `right_side`: custom normal-like values. `destination`: A permutation of all cells. Devices are ordered along the curve with curve slowest; every cell's new device is its old device or the one just before or after it. From each device at most 64 cells go to the next device and exactly as many come back from it; 64 is reached at some pair of neighbouring devices in every draw. `neighbour`: values below 512 are local cells of the same device. Only face 0 may name a slot from 512 to 512 + 256 - 1 (filled by the previous device from its send_list row 1), only face 1 a slot from 768 up (filled by the next device from its send_list row 0). Faces are paired: the cell across face f sees this cell across face f xor 1. -1 only at the domain boundary; the first device has no partner across its face 0 slots and the last none across face 1 slots. `orientation`: both sides of a shared face carry the same code; ignored where neighbour is -1. `send_list`: per device 256 distinct local cells in each row.
All inputs are finite; a program needn't handle non-finite values.
Results may differ from a plain program's by a relative error of at most 0.00015.
Values sent between devices are 32-bit elements; how exact they have to be, the bound alone decides.
A program may use at most 64 MiB of HBM per device.

v0:
```python
import functools

import jax
import jax.numpy as jnp
import numpy as np
from jax import lax
from jax.experimental import pallas as pl
from jax.experimental.pallas import tpu as pltpu
from jax.sharding import PartitionSpec as P

NODES = 5
BLOCK = 125
MOVE = 64
UNROLLED = 64
VMEM_LIMIT = 24 * 1024 * 1024
PENALTY = 80.0
MESH = pl.DeviceIdType.MESH
BF = jnp.bfloat16
F32 = jnp.float32

ROWS = 128
KAPPA = 125
TAG = 126
PART = 32
FACE = 2 * PART
FACE_KAPPA = 25
FACE_TAG = 26
HALO = PART + 24
FACE_LAST = 27

GAUSS_POINTS = (-0.906179845938664, -0.5384693101056831, 0.0, 0.5384693101056831, 0.906179845938664)
GAUSS_WEIGHTS = (
    0.2369268850561891,
    0.4786286704993665,
    0.5688888888888889,
    0.4786286704993665,
    0.2369268850561891,
)


def lagrange_value(points, position, location):
    out = 1.0
    for other in range(len(points)):
        if other != position:
            out = out * (location - points[other]) / (points[position] - points[other])
    return out


def lagrange_slope(points, position, location):
    total = 0.0
    for skipped in range(len(points)):
        if skipped == position:
            continue
        addend = 1.0 / (points[position] - points[skipped])
        for other in range(len(points)):
            if other != position and other != skipped:
                addend = addend * (location - points[other]) / (points[position] - points[other])
        total = total + addend
    return total


def along_axis(matrix, axis):
    five = np.eye(NODES)
    plane = np.eye(NODES * NODES)
    if axis == 0:
        return np.kron(matrix, plane)
    if axis == 1:
        return np.kron(five, np.kron(matrix, five))
    return np.kron(plane, matrix)


def split_table(table):
    high = table.astype(BF)
    low = (table - high.astype(np.float64)).astype(BF)
    return high, low


def tables():
    points = [0.5 * (value + 1.0) for value in GAUSS_POINTS]
    weights = np.array([0.5 * value for value in GAUSS_WEIGHTS])
    slopes = np.array([[lagrange_slope(points, p, points[q]) for p in range(NODES)] for q in range(NODES)])
    ends = [np.array([lagrange_value(points, p, at) for p in range(NODES)]) for at in (0.0, 1.0)]
    normals = [
        np.array([sign * lagrange_slope(points, p, at) for p in range(NODES)])
        for sign, at in ((-1.0, 0.0), (1.0, 1.0))
    ]
    cell_weight = np.kron(weights, np.kron(weights, weights))
    stiffness = np.zeros((BLOCK, BLOCK))
    for axis in range(3):
        grad = along_axis(slopes, axis)
        stiffness += grad.T @ (cell_weight[:, None] * grad)
    half = np.sqrt(0.5)
    parity_rows = np.zeros((NODES, NODES))
    for row, (a, b, sign) in enumerate(((0, 4, 1), (1, 3, 1), (2, 2, 1), (0, 4, -1), (1, 3, -1))):
        if a == b:
            parity_rows[row, a] = 1.0
        else:
            parity_rows[row, a] = half
            parity_rows[row, b] = sign * half
    parity = np.array([0, 0, 0, 1, 1])
    row_weight = weights[[0, 1, 2, 0, 1]]
    both = np.kron(parity_rows, parity_rows)
    count = NODES * NODES
    trace = np.zeros((6 * FACE, ROWS))
    for face in range(6):
        start = face * FACE
        trace[start : start + count, :BLOCK] = both @ along_axis(ends[face % 2][None, :], face // 2)
        trace[start + PART : start + PART + count, :BLOCK] = both @ along_axis(
            normals[face % 2][None, :], face // 2
        )
    lift = trace.T.copy()
    for face in range(6):
        trace[face * FACE + FACE_KAPPA, KAPPA] = 1.0
    first = np.zeros((6 * FACE + ROWS, ROWS))
    first[: 6 * FACE] = trace
    first[6 * FACE : 6 * FACE + BLOCK, :BLOCK] = stiffness
    high, low = split_table(first)
    forward = np.concatenate([high, high, low], 1)
    high, low = split_table(lift)
    backward = np.concatenate([high, low], 0)
    columns = np.zeros((ROWS, ROWS), np.float32)
    columns[:BLOCK, 0] = cell_weight
    columns[:count, 1] = np.kron(row_weight, row_weight)
    columns[:count, 2] = 2.0 * np.kron(parity, np.ones(NODES))
    columns[:count, 3] = 2.0 * np.kron(np.ones(NODES), parity)
    return forward, backward, columns


def split_two(value):
    high = value.astype(BF)
    low = (value - high.astype(F32)).astype(BF)
    return high, low


def split_three(value):
    high = value.astype(BF)
    rest = value - high.astype(F32)
    mid = rest.astype(BF)
    return high, mid, (rest - mid.astype(F32)).astype(BF)


def one_hot(left, right):
    return jnp.where(left == right, 1.0, 0.0).astype(BF)


def dot(left, right):
    return jnp.dot(left, right, preferred_element_type=F32)


def dot_last(left, right):
    return lax.dot_general(left, right, (((1,), (1,)), ((), ())), preferred_element_type=F32)


def iota(shape, dim):
    return lax.broadcasted_iota(jnp.int32, shape, dim)


def kernel(
    shape,
    rhs_hbm,
    cond_hbm,
    dest_hbm,
    neigh_hbm,
    orient_hbm,
    list_hbm,
    forward_hbm,
    backward_hbm,
    column_hbm,
    basis_hbm,
    linear_ref,
    square_ref,
    rhs_ref,
    cond_ref,
    dest_ref,
    neigh_ref,
    orient_ref,
    list_ref,
    forward_ref,
    backward_ref,
    column_ref,
    basis,
    payload,
    local_hot,
    ghost_hot,
    send_hot,
    packed,
    moved,
    far_out,
    far_in,
    halo_out,
    halo_in,
    sums,
    load_sem,
    store_sem,
    move_send,
    move_recv,
    far_send,
    far_recv,
    halo_send,
    halo_recv,
    sum_send,
    sum_recv,
):
    curve, group = shape
    ranks = curve * group
    cells = rhs_ref.shape[1]
    ghost = list_ref.shape[1]
    me = lax.axis_index("curve") * group + lax.axis_index("group")

    def place(rank):
        return (rank // group, lax.rem(rank, group))

    def other(step):
        return place(lax.rem(me + step, ranks))

    barrier = pltpu.get_barrier_semaphore()

    my_curve, my_group = lax.axis_index("curve"), lax.axis_index("group")

    def for_each_other(act):
        def order(count):
            return sorted(range(count), key=lambda step: -min(step, count - step))

        for curve_step in order(curve):
            to_curve = lax.rem(my_curve + curve_step, curve)

            def one(group_step):
                to_group = lax.rem(my_group + group_step, group)
                act(curve_step * group + group_step, (to_curve, to_group))

            if ranks <= UNROLLED:
                for group_step in order(group):
                    if curve_step or group_step:
                        one(group_step)
            else:
                pl.loop(0 if curve_step else 1, group)(one)

    for_each_other(
        lambda _, device: pl.semaphore_signal(barrier, inc=1, device_id=device, device_id_type=MESH)
    )

    loads = [
        pltpu.make_async_copy(source, target, load_sem.at[index])
        for index, (source, target) in enumerate(
            (
                (dest_hbm, dest_ref),
                (list_hbm, list_ref),
                (cond_hbm, cond_ref),
                (rhs_hbm, rhs_ref),
                (forward_hbm, forward_ref),
                (neigh_hbm, neigh_ref),
                (orient_hbm, orient_ref),
                (column_hbm, column_ref),
                (backward_hbm, backward_ref),
            )
        )
    ]
    for load in loads:
        load.start()
    for load in loads[:4]:
        load.wait()

    def faces_of(stacked, kappa, first, last):
        part = dot(forward_ref[first * FACE : last * FACE, :], stacked)
        own, halves = [], []
        for index in range(last - first):
            value = part[index * FACE : index * FACE + PART]
            flux = kappa * part[index * FACE + PART : (index + 1) * FACE]
            own.append((value, flux))
            halves.append(jnp.concatenate(split_two(jnp.concatenate([value, flux], 0)), 0))
        return own, halves

    offset = dest_ref[...] - me * cells
    goes_left = offset < 0
    goes_right = offset >= cells
    slot = jnp.where(goes_left, offset + cells, jnp.where(goes_right, offset - cells, offset))
    payload[0:BLOCK, :] = rhs_ref[...]
    payload[KAPPA : KAPPA + 1, :] = cond_ref[...]
    payload[TAG : TAG + 1, :] = (slot + 1).astype(F32)
    payload[TAG + 1 : TAG + 2, :] = jnp.zeros((1, cells), F32)
    high, mid, low = split_three(payload[...])
    parts = jnp.concatenate([high, mid, low], 0)
    row8 = iota((8, cells), 0)
    leaving = jnp.where(
        row8 == 0,
        jnp.where(goes_left, 1.0, 0.0),
        jnp.where(row8 == 1, jnp.where(goes_right, 1.0, 0.0), 0.0),
    ).astype(BF)
    triangle = jnp.where(iota((cells, cells), 0) <= iota((cells, cells), 1), 1.0, 0.0).astype(BF)
    order = dot(leaving, triangle).astype(jnp.int32) - 1
    slots = iota((MOVE, cells), 0)
    pick = jnp.concatenate(
        [
            one_hot(jnp.where(goes_left, order[0:1], -1), slots),
            one_hot(jnp.where(goes_right, order[1:2], -1), slots),
        ],
        0,
    )
    chosen = dot_last(pick, parts)
    chosen = chosen[:, :ROWS] + chosen[:, ROWS : 2 * ROWS] + chosen[:, 2 * ROWS :]
    packed[0] = chosen[:MOVE]
    packed[1] = chosen[MOVE:]

    pl.semaphore_wait(barrier, ranks - 1)

    def exchange(source, target, send_sem, recv_sem, reach):
        return [
            pltpu.make_async_remote_copy(
                src_ref=source.at[side],
                dst_ref=target.at[1 - side],
                send_sem=send_sem.at[side],
                recv_sem=recv_sem.at[1 - side],
                device_id=device,
                device_id_type=MESH,
            )
            for side, device in ((0, other(ranks - reach)), (1, other(reach)))
        ]

    moves = exchange(packed, moved, move_send, move_recv, 1)
    for copy in moves:
        copy.start()

    for load in loads[4:]:
        load.wait()

    old_halves = faces_of(jnp.concatenate([high, mid, high], 0), cond_ref[...], 0, 2)[1]
    offset_column = jnp.broadcast_to(offset.astype(F32), (8, cells)).T[:, 0:1]
    lists = list_ref[...].astype(F32)
    halo_rows = iota((HALO, ghost), 0)

    def shrink(out):
        out = out[:FACE] + out[FACE:]
        return jnp.where(halo_rows == FACE_LAST, out[HALO : HALO + 1], out[:HALO])

    def widen(message):
        last = message[FACE_LAST : FACE_LAST + 1]
        rest = jnp.where(iota((FACE - HALO, ghost), 0) == 0, last, 0.0)
        return jnp.concatenate([message, rest], 0)

    for side in range(2):
        hot = one_hot(offset_column, lists[side : side + 1, :])
        out = dot(old_halves[side], hot)
        halo_out[0, side] = jnp.where(
            halo_rows == FACE_TAG, lists[side : side + 1, :], shrink(out)
        )
    lanes = iota((2 * MOVE, ROWS), 1)
    tagged = jnp.where(lanes == FACE_TAG, chosen[:, TAG : TAG + 1], 0.0)
    leaving_low = dot_last(pick, old_halves[0]) + tagged
    leaving_high = dot_last(pick, old_halves[1]) + tagged
    leaving_low = leaving_low[:, :FACE] + leaving_low[:, FACE:]
    leaving_high = leaving_high[:, :FACE] + leaving_high[:, FACE:]
    middle = MOVE // 2
    far_out[0] = jnp.concatenate([leaving_low[:middle], leaving_low[middle:MOVE]], 1)
    far_out[1] = jnp.concatenate([leaving_high[MOVE : MOVE + middle], leaving_high[MOVE + middle :]], 1)

    halos = exchange(halo_out.at[0], halo_in.at[0], halo_send.at[0], halo_recv.at[0], 1)
    fars = exchange(far_out, far_in, far_send, far_recv, 2)
    for copy in fars + halos:
        copy.start()

    stay = one_hot(iota((cells, cells), 0), offset)
    arrived = dot_last(parts, stay)
    cell_rows = iota((cells, cells), 0)
    ghost_rows = iota((ghost, cells), 0)
    for face in range(6):
        local_hot[face] = one_hot(neigh_ref[face : face + 1, :], cell_rows)
    for side in range(2):
        ghost_hot[side] = one_hot(
            neigh_ref[side : side + 1, :] - (cells + side * ghost), ghost_rows
        )
        send_hot[side] = one_hot(list_ref[side : side + 1, :], iota((cells, ghost), 0))

    for copy in moves:
        copy.wait()
    record = moved[...].reshape(2 * MOVE, ROWS)
    landing = record[:, TAG : TAG + 1].astype(jnp.int32) - 1
    record_parts = jnp.concatenate(split_three(record.T), 0)
    arrived = arrived + dot(record_parts, one_hot(landing, iota((2 * MOVE, cells), 1)))
    arrived = arrived[:ROWS] + arrived[ROWS : 2 * ROWS] + arrived[2 * ROWS :]
    rows = iota((ROWS, cells), 0)
    field = jnp.where(rows < BLOCK, arrived, 0.0)
    kappa = arrived[KAPPA : KAPPA + 1]
    cell_weight = column_ref[:, 0:1]
    face_weight = column_ref[0:PART, 1:2]
    first_odd = column_ref[0:PART, 2:3]
    second_odd = column_ref[0:PART, 3:4]

    def operate(field, turn, between):
        high, low = split_two(jnp.where(rows == KAPPA, kappa, field))
        stacked = jnp.concatenate([high, low, high], 0)
        own, halves = faces_of(stacked, kappa, 0, 2)
        copies = halos + fars
        if turn:
            for side in range(2):
                out = dot(halves[side], send_hot[side])
                halo_out[turn, side] = shrink(out)
            copies = exchange(
                halo_out.at[turn], halo_in.at[turn], halo_send.at[turn], halo_recv.at[turn], 1
            )
            for copy in copies:
                copy.start()
        more_own, more_halves = faces_of(stacked, kappa, 2, 6)
        own, halves = own + more_own, halves + more_halves

        def coefficients(face, near):
            value, flux = own[face]
            code = orient_ref[face : face + 1, :]
            first_bit = jnp.where(lax.rem(code, 2) == 1, 1.0, 0.0)
            second_bit = jnp.where(code >= 2, 1.0, 0.0)
            sign = (1.0 - first_odd * first_bit) * (1.0 - second_odd * second_bit)
            outside = jnp.where(neigh_ref[face : face + 1, :] < 0, 1.0, 0.0)
            near = near[:FACE] + near[FACE:]
            near_kappa = near[FACE_KAPPA : FACE_KAPPA + 1] + outside * kappa
            penalty = PENALTY * jnp.maximum(kappa, near_kappa)
            jump = value - (sign * near[:PART] - outside * value)
            mean = flux - (sign * near[PART:] - outside * flux)
            scaled = -0.5 * (face_weight * jump)
            return face_weight * (penalty * jump - 0.5 * mean), kappa * scaled, scaled

        def lifted(terms, first, last):
            high, low = split_two(jnp.concatenate(terms, 0))
            both = dot(backward_ref[:, first * FACE : last * FACE], high)
            rest = dot(backward_ref[0:ROWS, first * FACE : last * FACE], low)
            return both[:ROWS] + both[ROWS:] + rest

        terms = []
        for face in range(2, 6):
            terms += coefficients(face, dot(halves[face ^ 1], local_hot[face]))[:2]
        result = lifted(terms, 2, 6)
        stiff = dot(forward_ref[6 * FACE :, :], stacked)
        result = result + cell_weight * field + kappa * stiff
        near = [dot(halves[face ^ 1], local_hot[face]) for face in range(2)]
        between(result)
        for copy in copies:
            copy.wait()
        terms, energy = [], 0.0
        for face in range(2):
            ghosts = widen(halo_in[turn, face])
            if not turn:
                gone = leaving_high[:MOVE] if face == 0 else leaving_low[MOVE:]
                far = far_in[face]
                wide = jnp.concatenate([far[:, :FACE], far[:, FACE:], gone], 0)
                hot = one_hot(wide[:, FACE_TAG : FACE_TAG + 1] - 1.0, ghosts[FACE_TAG : FACE_TAG + 1])
                placed = dot(jnp.concatenate(split_two(wide.T), 0), hot)
                ghosts = ghosts + placed[:FACE] + placed[FACE:]
            received = jnp.concatenate(split_two(ghosts), 0)
            first, second, scaled = coefficients(face, near[face] + dot(received, ghost_hot[face]))
            terms += [first, second]
            energy = energy + jnp.sum(own[face][0] * first + own[face][1] * scaled, 0, keepdims=True)
        return result, energy, lambda: lifted(terms, 0, 2)

    def down(value):
        return jnp.sum(value, 0, keepdims=True)

    def across(value):
        return jnp.sum(value, 1, keepdims=True)

    def save(index, value):
        basis[index] = value
        return pltpu.make_async_copy(basis.at[index], basis_hbm.at[index], store_sem.at[index])

    stores = [save(0, field)]
    stores[0].start()
    result, _, lift = operate(field, 0, lambda result: None)
    image = result + lift()
    stores.append(save(1, image))
    stores[1].start()
    found = []

    def early_sums(result):
        found.append(across(down(field * field)))
        found.append(across(down(field * image)))
        found.append(across(down(image * image)))
        found.append(down(image * result))

    result, energy, lift = operate(image, 1, early_sums)
    found[3] = across(found[3] + energy)

    lane = iota((1, ROWS), 1)
    message = jnp.zeros((1, ROWS), F32)
    for index, value in enumerate(found):
        message = jnp.where(lane == index, value, message)
    sums[0] = message

    for_each_other(
        lambda index, device: pltpu.make_async_remote_copy(
            src_ref=sums.at[0],
            dst_ref=sums.at[index],
            send_sem=sum_send,
            recv_sem=sum_recv,
            device_id=device,
            device_id_type=MESH,
        ).start()
    )

    stores.append(save(2, result + lift()))
    stores[2].start()
    rest = sums.at[pl.ds(1, ranks - 1)]
    pltpu.make_async_copy(rest, rest, sum_send).wait()
    pltpu.make_async_copy(rest, rest, sum_recv).wait()
    summed = jnp.sum(sums[...], 0)
    s00, s01, s11, s12 = (summed[:, index : index + 1] for index in range(4))
    first_step = s00 / s01
    next_norm = s00 - 2.0 * first_step * s01 + first_step * first_step * s11
    inner = s01 - 2.0 * first_step * s11 + first_step * first_step * s12
    beta = next_norm / s00
    second_step = next_norm / (inner - beta * next_norm / first_step)
    linear = first_step + second_step * (1.0 + beta)
    square = first_step * second_step
    linear_ref[...] = jnp.broadcast_to(linear, (1, cells))
    square_ref[...] = jnp.broadcast_to(square, (1, cells))
    for store in stores:
        store.wait()


def body(shape, right_side, conductivity, destination, neighbour, orientation, send_list):
    cells = right_side.shape[1]
    ghost = send_list.shape[1]
    ranks = shape[0] * shape[1]
    forward, backward, columns = tables()
    vmem = pl.BlockSpec(memory_space=pltpu.VMEM)
    anywhere = pl.BlockSpec(memory_space=pl.ANY)
    dma = pltpu.SemaphoreType.DMA
    operands = (
        right_side,
        conductivity[None],
        destination[None],
        neighbour,
        orientation,
        send_list,
        jnp.asarray(forward),
        jnp.asarray(backward),
        jnp.asarray(columns),
    )
    operands = tuple(pltpu.with_memory_space_constraint(item, pltpu.HBM) for item in operands)
    basis, linear, square = pl.pallas_call(
        functools.partial(kernel, shape),
        out_shape=(
            jax.ShapeDtypeStruct((3, ROWS, cells), F32),
            jax.ShapeDtypeStruct((1, cells), F32),
            jax.ShapeDtypeStruct((1, cells), F32),
        ),
        in_specs=[pl.BlockSpec(memory_space=pltpu.HBM)] * len(operands),
        out_specs=(anywhere, vmem, vmem),
        scratch_shapes=[pltpu.VMEM(item.shape, item.dtype) for item in operands]
        + [
            pltpu.VMEM((3, ROWS, cells), F32),
            pltpu.VMEM((ROWS, cells), F32),
            pltpu.VMEM((6, cells, cells), BF),
            pltpu.VMEM((2, ghost, cells), BF),
            pltpu.VMEM((2, cells, ghost), BF),
            pltpu.VMEM((2, MOVE, ROWS), F32),
            pltpu.VMEM((2, MOVE, ROWS), F32),
            pltpu.VMEM((2, MOVE // 2, ROWS), F32),
            pltpu.VMEM((2, MOVE // 2, ROWS), F32),
            pltpu.VMEM((2, 2, HALO, ghost), F32),
            pltpu.VMEM((2, 2, HALO, ghost), F32),
            pltpu.VMEM((ranks, 1, ROWS), F32),
            dma((len(operands),)),
            dma((3,)),
            dma((2,)),
            dma((2,)),
            dma((2,)),
            dma((2,)),
            dma((2, 2)),
            dma((2, 2)),
            dma,
            dma,
        ],
        compiler_params=pltpu.CompilerParams(
            collective_id=0, has_side_effects=True, vmem_limit_bytes=VMEM_LIMIT
        ),
    )(*operands)
    first, second, third = (basis[index, :BLOCK] for index in range(3))
    return linear * first - square * second, first - linear * second + square * third


def solution(mesh):
    both = ("curve", "group")
    shape = (mesh.shape["curve"], mesh.shape["group"])
    in_specs = (P(None, both), P(both), P(both), P(None, both), P(None, both), P(None, both))
    out_specs = (P(None, both), P(None, both))
    return jax.shard_map(
        functools.partial(body, shape),
        mesh=mesh,
        in_specs=in_specs,
        out_specs=out_specs,
        check_vma=False,
    )
```

profile of v0, /device:TPU:0, one launch (start us, length us, event | category | flops | bytes accessed | tf_op | source)
XLA Modules:
  0.0 25.2 jit_solution(11407972944273594645)
XLA Ops:
  0.6 23.7 %shard_map.104 = (f32[3,128,512]{2,1,0:T(8,128)S(1)}, f32[1,512]{1,0:T(1,128)S(1)}, f32[1,512]{1,0:T(1,128)S(1)}) custom-call(f32[125,512]{1,0:T(8,128)} %rhs_hbm.1, f32[1,512]{1,0:T(1,128)} %bitcast.24, s32[1,512]{1,0:T(1,128)} %bitcast.25, s32[6,512]{1,0:T(8,128)} %neigh_hbm.1, s32[6,512]{1,0:T(8,128)} %orient_hbm.1, s32[2,256]{1,0:T(2,128)} %list_hbm.1, ...), custom_call_target="tpu_custom_call" | custom-call | tf_op jit(solution)/shard_map/pallas_call | solution.py:536
  24.3 0.9 %fusion = (f32[125,512]{1,0:T(8,128)}, f32[125,512]{1,0:T(8,128)}) fusion(f32[3,128,512]{2,1,0:T(8,128)S(1)} %get-tuple-element.6, f32[512]{0:T(512)S(1)} %bitcast.23, f32[512]{0:T(512)S(1)} %bitcast.22), kind=kLoop, calls=%fused_computation.1 | loop fusion | flops 448000 | bytes 1284096 | tf_op jit(solution)/shard_map/add | solution.py:575
where the time goes:
time: 25.4 us; the launch traced here: 25.2 us
  Pallas kernels  23.7 us (93%)
  other arithmetic  0.88 us (3%)
  between operations  0.64 us (3%)
    pallas_call x1, Pallas kernels, body(): pl.pallas_call(functools.partial(kernel, shape), out_shape=(jax.ShapeDtyp...  23.7 us
    add x1, other arithmetic, body(): first - linear * second + square * third  0.88 us

commit v1 on v0

--- a/solution.py
+++ b/solution.py
@@ -166,7 +166,7 @@
     forward_hbm,
     backward_hbm,
     column_hbm,
-    basis_hbm,
+    basis,
     linear_ref,
     square_ref,
     rhs_ref,
@@ -178,7 +178,6 @@
     forward_ref,
     backward_ref,
     column_ref,
-    basis,
     payload,
     local_hot,
     ghost_hot,
@@ -190,8 +189,8 @@
     halo_out,
     halo_in,
     sums,
+    kept,
     load_sem,
-    store_sem,
     move_send,
     move_recv,
     far_send,
@@ -213,30 +212,61 @@
     def other(step):
         return place(lax.rem(me + step, ranks))
 
+    class Exchange:
+        def __init__(self, source, target, send_sem, recv_sem, reach):
+            self.there = (me >= reach, me + reach < ranks)
+            self.copies = [
+                pltpu.make_async_remote_copy(
+                    src_ref=source.at[side],
+                    dst_ref=target.at[1 - side],
+                    send_sem=send_sem.at[side],
+                    recv_sem=recv_sem.at[1 - side],
+                    device_id=device,
+                    device_id_type=MESH,
+                )
+                for side, device in ((0, other(ranks - reach)), (1, other(reach)))
+            ]
+
+        def start(self):
+            for side in range(2):
+                pl.when(self.there[side])(self.copies[side].start)
+
+        def arrive(self, side):
+            pl.when(self.there[side])(self.copies[1 - side].wait_recv)
+
+        def leave(self):
+            for side in range(2):
+                pl.when(self.there[side])(self.copies[side].wait_send)
+
+    def clear(reach, refs):
+        for side, missing in ((0, me < reach), (1, me + reach >= ranks)):
+
+            @pl.when(missing)
+            def _():
+                for ref in refs:
+                    ref[side] = jnp.zeros(ref.shape[1:], ref.dtype)
+
     barrier = pltpu.get_barrier_semaphore()
 
     my_curve, my_group = lax.axis_index("curve"), lax.axis_index("group")
 
     def for_each_other(act):
-        def order(count):
-            return sorted(range(count), key=lambda step: -min(step, count - step))
-
-        for curve_step in order(curve):
-            to_curve = lax.rem(my_curve + curve_step, curve)
-
-            def one(group_step):
-                to_group = lax.rem(my_group + group_step, group)
-                act(curve_step * group + group_step, (to_curve, to_group))
-
-            if ranks <= UNROLLED:
-                for group_step in order(group):
-                    if curve_step or group_step:
-                        one(group_step)
-            else:
-                pl.loop(0 if curve_step else 1, group)(one)
+        def one(to_group):
+            for step in range(curve):
+                to = (lax.rem(my_curve + step, curve), to_group)
+                if step:
+                    act(to)
+                else:
+                    pl.when(to_group != my_group)(functools.partial(act, to))
+
+        if ranks <= UNROLLED:
+            for to_group in range(group):
+                one(to_group)
+        else:
+            pl.loop(0, group)(one)
 
     for_each_other(
-        lambda _, device: pl.semaphore_signal(barrier, inc=1, device_id=device, device_id_type=MESH)
+        lambda device: pl.semaphore_signal(barrier, inc=1, device_id=device, device_id_type=MESH)
     )
 
     loads = [
@@ -257,6 +287,8 @@
     ]
     for load in loads:
         load.start()
+    clear(1, (moved, halo_in.at[0], halo_in.at[1]))
+    clear(2, (far_in,))
     for load in loads[:4]:
         load.wait()
 
@@ -303,22 +335,8 @@
 
     pl.semaphore_wait(barrier, ranks - 1)
 
-    def exchange(source, target, send_sem, recv_sem, reach):
-        return [
-            pltpu.make_async_remote_copy(
-                src_ref=source.at[side],
-                dst_ref=target.at[1 - side],
-                send_sem=send_sem.at[side],
-                recv_sem=recv_sem.at[1 - side],
-                device_id=device,
-                device_id_type=MESH,
-            )
-            for side, device in ((0, other(ranks - reach)), (1, other(reach)))
-        ]
-
-    moves = exchange(packed, moved, move_send, move_recv, 1)
-    for copy in moves:
-        copy.start()
+    moves = Exchange(packed, moved, move_send, move_recv, 1)
+    moves.start()
 
     for load in loads[4:]:
         load.wait()
@@ -353,10 +371,10 @@
     far_out[0] = jnp.concatenate([leaving_low[:middle], leaving_low[middle:MOVE]], 1)
     far_out[1] = jnp.concatenate([leaving_high[MOVE : MOVE + middle], leaving_high[MOVE + middle :]], 1)
 
-    halos = exchange(halo_out.at[0], halo_in.at[0], halo_send.at[0], halo_recv.at[0], 1)
-    fars = exchange(far_out, far_in, far_send, far_recv, 2)
-    for copy in fars + halos:
-        copy.start()
+    halos = Exchange(halo_out.at[0], halo_in.at[0], halo_send.at[0], halo_recv.at[0], 1)
+    fars = Exchange(far_out, far_in, far_send, far_recv, 2)
+    fars.start()
+    halos.start()
 
     stay = one_hot(iota((cells, cells), 0), offset)
     arrived = dot_last(parts, stay)
@@ -370,8 +388,8 @@
         )
         send_hot[side] = one_hot(list_ref[side : side + 1, :], iota((cells, ghost), 0))
 
-    for copy in moves:
-        copy.wait()
+    for side in range(2):
+        moves.arrive(side)
     record = moved[...].reshape(2 * MOVE, ROWS)
     landing = record[:, TAG : TAG + 1].astype(jnp.int32) - 1
     record_parts = jnp.concatenate(split_three(record.T), 0)
@@ -385,69 +403,51 @@
     first_odd = column_ref[0:PART, 2:3]
     second_odd = column_ref[0:PART, 3:4]
 
-    def operate(field, turn, between):
+    def signs(face):
+        code = orient_ref[face : face + 1, :]
+        first_bit = jnp.where(lax.rem(code, 2) == 1, 1.0, 0.0)
+        second_bit = jnp.where(code >= 2, 1.0, 0.0)
+        return (1.0 - first_odd * first_bit) * (1.0 - second_odd * second_bit)
+
+    def outer(face):
+        return jnp.where(neigh_ref[face : face + 1, :] < 0, 1.0, 0.0)
+
+    def coefficients(face, own, near):
+        value, flux = own
+        sign = signs(face)
+        outside = outer(face)
+        near = near[:FACE] + near[FACE:]
+        near_kappa = near[FACE_KAPPA : FACE_KAPPA + 1] + outside * kappa
+        penalty = PENALTY * jnp.maximum(kappa, near_kappa)
+        jump = value - (sign * near[:PART] - outside * value)
+        mean = flux - (sign * near[PART:] - outside * flux)
+        scaled = -0.5 * (face_weight * jump)
+        first = face_weight * (penalty * jump - 0.5 * mean)
+        return (first, kappa * scaled), (jump, mean, first, scaled)
+
+    def lifted(terms, first, last):
+        high, low = split_two(jnp.concatenate(terms, 0))
+        both = dot(backward_ref[:, first * FACE : last * FACE], high)
+        rest = dot(backward_ref[0:ROWS, first * FACE : last * FACE], low)
+        return both[:ROWS] + both[ROWS:] + rest
+
+    def stack(field):
         high, low = split_two(jnp.where(rows == KAPPA, kappa, field))
-        stacked = jnp.concatenate([high, low, high], 0)
-        own, halves = faces_of(stacked, kappa, 0, 2)
-        copies = halos + fars
-        if turn:
-            for side in range(2):
-                out = dot(halves[side], send_hot[side])
-                halo_out[turn, side] = shrink(out)
-            copies = exchange(
-                halo_out.at[turn], halo_in.at[turn], halo_send.at[turn], halo_recv.at[turn], 1
-            )
-            for copy in copies:
-                copy.start()
+        return jnp.concatenate([high, low, high], 0)
+
+    def inner(field, stacked, halves):
         more_own, more_halves = faces_of(stacked, kappa, 2, 6)
-        own, halves = own + more_own, halves + more_halves
-
-        def coefficients(face, near):
-            value, flux = own[face]
-            code = orient_ref[face : face + 1, :]
-            first_bit = jnp.where(lax.rem(code, 2) == 1, 1.0, 0.0)
-            second_bit = jnp.where(code >= 2, 1.0, 0.0)
-            sign = (1.0 - first_odd * first_bit) * (1.0 - second_odd * second_bit)
-            outside = jnp.where(neigh_ref[face : face + 1, :] < 0, 1.0, 0.0)
-            near = near[:FACE] + near[FACE:]
-            near_kappa = near[FACE_KAPPA : FACE_KAPPA + 1] + outside * kappa
-            penalty = PENALTY * jnp.maximum(kappa, near_kappa)
-            jump = value - (sign * near[:PART] - outside * value)
-            mean = flux - (sign * near[PART:] - outside * flux)
-            scaled = -0.5 * (face_weight * jump)
-            return face_weight * (penalty * jump - 0.5 * mean), kappa * scaled, scaled
-
-        def lifted(terms, first, last):
-            high, low = split_two(jnp.concatenate(terms, 0))
-            both = dot(backward_ref[:, first * FACE : last * FACE], high)
-            rest = dot(backward_ref[0:ROWS, first * FACE : last * FACE], low)
-            return both[:ROWS] + both[ROWS:] + rest
-
         terms = []
         for face in range(2, 6):
-            terms += coefficients(face, dot(halves[face ^ 1], local_hot[face]))[:2]
+            near = dot(more_halves[(face ^ 1) - 2], local_hot[face])
+            terms += coefficients(face, more_own[face - 2], near)[0]
         result = lifted(terms, 2, 6)
         stiff = dot(forward_ref[6 * FACE :, :], stacked)
         result = result + cell_weight * field + kappa * stiff
-        near = [dot(halves[face ^ 1], local_hot[face]) for face in range(2)]
-        between(result)
-        for copy in copies:
-            copy.wait()
-        terms, energy = [], 0.0
-        for face in range(2):
-            ghosts = widen(halo_in[turn, face])
-            if not turn:
-                gone = leaving_high[:MOVE] if face == 0 else leaving_low[MOVE:]
-                far = far_in[face]
-                wide = jnp.concatenate([far[:, :FACE], far[:, FACE:], gone], 0)
-                hot = one_hot(wide[:, FACE_TAG : FACE_TAG + 1] - 1.0, ghosts[FACE_TAG : FACE_TAG + 1])
-                placed = dot(jnp.concatenate(split_two(wide.T), 0), hot)
-                ghosts = ghosts + placed[:FACE] + placed[FACE:]
-            received = jnp.concatenate(split_two(ghosts), 0)
-            first, second, scaled = coefficients(face, near[face] + dot(received, ghost_hot[face]))
-            terms += [first, second]
-            energy = energy + jnp.sum(own[face][0] * first + own[face][1] * scaled, 0, keepdims=True)
-        return result, energy, lambda: lifted(terms, 0, 2)
+        return result, [dot(halves[face ^ 1], local_hot[face]) for face in range(2)]
+
+    def with_ghosts(near, ghosts, side):
+        return near + dot(jnp.concatenate(split_two(ghosts), 0), ghost_hot[side])
 
     def down(value):
         return jnp.sum(value, 0, keepdims=True)
@@ -455,37 +455,71 @@
     def across(value):
         return jnp.sum(value, 1, keepdims=True)
 
-    def save(index, value):
-        basis[index] = value
-        return pltpu.make_async_copy(basis.at[index], basis_hbm.at[index], store_sem.at[index])
-
-    stores = [save(0, field)]
-    stores[0].start()
-    result, _, lift = operate(field, 0, lambda result: None)
-    image = result + lift()
-    stores.append(save(1, image))
-    stores[1].start()
-    found = []
-
-    def early_sums(result):
-        found.append(across(down(field * field)))
-        found.append(across(down(field * image)))
-        found.append(across(down(image * image)))
-        found.append(down(image * result))
-
-    result, energy, lift = operate(image, 1, early_sums)
-    found[3] = across(found[3] + energy)
-
+    basis[0] = field
+    stacked = stack(field)
+    own, halves = faces_of(stacked, kappa, 0, 2)
+    result, near = inner(field, stacked, halves)
+    for side in range(2):
+        halos.arrive(side)
+        fars.arrive(side)
+    terms = []
+    for face in range(2):
+        ghosts = widen(halo_in[0, face])
+        gone = leaving_high[:MOVE] if face == 0 else leaving_low[MOVE:]
+        far = far_in[face]
+        wide = jnp.concatenate([far[:, :FACE], far[:, FACE:], gone], 0)
+        hot = one_hot(wide[:, FACE_TAG : FACE_TAG + 1] - 1.0, ghosts[FACE_TAG : FACE_TAG + 1])
+        placed = dot(jnp.concatenate(split_two(wide.T), 0), hot)
+        ghosts = ghosts + placed[:FACE] + placed[FACE:]
+        terms += coefficients(face, own[face], with_ghosts(near[face], ghosts, face))[0]
+    image = result + lifted(terms, 0, 2)
+
+    stacked = stack(image)
+    own, halves = faces_of(stacked, kappa, 0, 2)
+    for side in range(2):
+        halo_out[1, side] = shrink(dot(halves[side], send_hot[side]))
+    images = Exchange(halo_out.at[1], halo_in.at[1], halo_send.at[1], halo_recv.at[1], 1)
+    images.start()
+    basis[1] = image
+    result, near = inner(image, stacked, halves)
+    value, flux = own[1]
+    edge = 2.0 * outer(1) * down(face_weight * (value * (PENALTY * kappa * value - flux)))
+    found = [across(down(field * field)), across(down(field * image)), across(down(image * image))]
+    outside = outer(0) > 0.0
+    kept[...] = near[0]
+    _, (jump, mean, first, scaled) = coefficients(0, own[0], near[0])
+
+    inside = jnp.where(outside, own[0][0], jump) * first + jnp.where(outside, own[0][1], mean) * scaled
+    inside = jnp.where(neigh_ref[0:1, :] < cells, down(inside), 0.0)
+    found.append(across(down(image * result) + edge + inside))
     lane = iota((1, ROWS), 1)
     message = jnp.zeros((1, ROWS), F32)
     for index, value in enumerate(found):
         message = jnp.where(lane == index, value, message)
-    sums[0] = message
+    across_edge = dot_last(halves[0], ghost_hot[0])
+    across_edge = across_edge[:FACE] + across_edge[FACE:]
+    code = orient_ref[0:1, :]
+    bit_rows = iota((8, cells), 0)
+    bits = jnp.where(
+        bit_rows == 0, lax.rem(code, 2), jnp.where(bit_rows == 1, jnp.where(code >= 2, 1, 0), 1)
+    )
+    bits = dot_last(bits.astype(F32).astype(BF), ghost_hot[0])
+    slot_sign = (1.0 - first_odd * bits[0:1]) * (1.0 - second_odd * bits[1:2])
+    slot_weight = face_weight * bits[2:3]
+    slot_kappa = across_edge[FACE_KAPPA : FACE_KAPPA + 1]
+
+    images.arrive(0)
+    ghosts = widen(halo_in[1, 0])
+    penalty = PENALTY * jnp.maximum(slot_kappa, ghosts[FACE_KAPPA : FACE_KAPPA + 1])
+    jump = across_edge[:PART] - slot_sign * ghosts[:PART]
+    mean = across_edge[PART:] - slot_sign * ghosts[PART:]
+    shared = across(down(slot_weight * (jump * (penalty * jump - mean))))
+    sums[me] = message + jnp.where(lane == 3, shared, 0.0)
 
     for_each_other(
-        lambda index, device: pltpu.make_async_remote_copy(
-            src_ref=sums.at[0],
-            dst_ref=sums.at[index],
+        lambda device: pltpu.make_async_remote_copy(
+            src_ref=sums.at[me],
+            dst_ref=sums.at[me],
             send_sem=sum_send,
             recv_sem=sum_recv,
             device_id=device,
@@ -493,24 +527,25 @@
         ).start()
     )
 
-    stores.append(save(2, result + lift()))
-    stores[2].start()
+    images.arrive(1)
+    terms = []
+    near[0] = kept[...]
+    for face in range(2):
+        terms += coefficients(face, own[face], with_ghosts(near[face], widen(halo_in[1, face]), face))[0]
+    basis[2] = result + lifted(terms, 0, 2)
+    for copies in (moves, halos, fars, images):
+        copies.leave()
     rest = sums.at[pl.ds(1, ranks - 1)]
     pltpu.make_async_copy(rest, rest, sum_send).wait()
     pltpu.make_async_copy(rest, rest, sum_recv).wait()
     summed = jnp.sum(sums[...], 0)
-    s00, s01, s11, s12 = (summed[:, index : index + 1] for index in range(4))
-    first_step = s00 / s01
-    next_norm = s00 - 2.0 * first_step * s01 + first_step * first_step * s11
-    inner = s01 - 2.0 * first_step * s11 + first_step * first_step * s12
-    beta = next_norm / s00
-    second_step = next_norm / (inner - beta * next_norm / first_step)
-    linear = first_step + second_step * (1.0 + beta)
-    square = first_step * second_step
+    ratios = pltpu.roll(summed, ROWS - 1, 1) / summed
+    low, mid, high = (ratios[:, index : index + 1] for index in range(3))
+    scale = 1.0 / (low * mid * (high - mid))
+    linear = mid * (high - low) * scale
+    square = (mid - low) * scale
     linear_ref[...] = jnp.broadcast_to(linear, (1, cells))
     square_ref[...] = jnp.broadcast_to(square, (1, cells))
-    for store in stores:
-        store.wait()
 
 
 def body(shape, right_side, conductivity, destination, neighbour, orientation, send_list):
@@ -519,7 +554,6 @@
     ranks = shape[0] * shape[1]
     forward, backward, columns = tables()
     vmem = pl.BlockSpec(memory_space=pltpu.VMEM)
-    anywhere = pl.BlockSpec(memory_space=pl.ANY)
     dma = pltpu.SemaphoreType.DMA
     operands = (
         right_side,
@@ -541,10 +575,9 @@
             jax.ShapeDtypeStruct((1, cells), F32),
         ),
         in_specs=[pl.BlockSpec(memory_space=pltpu.HBM)] * len(operands),
-        out_specs=(anywhere, vmem, vmem),
+        out_specs=(vmem, vmem, vmem),
         scratch_shapes=[pltpu.VMEM(item.shape, item.dtype) for item in operands]
         + [
-            pltpu.VMEM((3, ROWS, cells), F32),
             pltpu.VMEM((ROWS, cells), F32),
             pltpu.VMEM((6, cells, cells), BF),
             pltpu.VMEM((2, ghost, cells), BF),
@@ -556,8 +589,8 @@
             pltpu.VMEM((2, 2, HALO, ghost), F32),
             pltpu.VMEM((2, 2, HALO, ghost), F32),
             pltpu.VMEM((ranks, 1, ROWS), F32),
+            pltpu.VMEM((2 * FACE, cells), F32),
             dma((len(operands),)),
-            dma((3,)),
             dma((2,)),
             dma((2,)),
             dma((2,)),

time: 25.4 us -> 25 us (0.984)
  Pallas kernels: 23.7 us -> 23.3 us
    pallas_call x1, Pallas kernels: 23.7 us -> 23.3 us  [body(): pl.pallas_call(functools.partial(kernel, shape), out_shape=(jax.ShapeDtyp...]
where the time goes in v1:
time: 25 us; the launch traced here: 24.8 us
  Pallas kernels  23.3 us (93%)
  other arithmetic  0.88 us (4%)
  between operations  0.64 us (3%)
    pallas_call x1, Pallas kernels, body(): pl.pallas_call(functools.partial(kernel, shape), out_shape=(jax.ShapeDtyp...  23.3 us
    add x1, other arithmetic, body(): first - linear * second + square * third  0.88 us

profile of v1, /device:TPU:0, one launch (start us, length us, event | category | flops | bytes accessed | tf_op | source)
XLA Modules:
  0.0 24.8 jit_solution(7084484737261137930)
XLA Ops:
  0.6 23.3 %shard_map.104 = (f32[3,128,512]{2,1,0:T(8,128)S(1)}, f32[1,512]{1,0:T(1,128)S(1)}, f32[1,512]{1,0:T(1,128)S(1)}) custom-call(f32[125,512]{1,0:T(8,128)} %rhs_hbm.1, f32[1,512]{1,0:T(1,128)} %bitcast.24, s32[1,512]{1,0:T(1,128)} %bitcast.25, s32[6,512]{1,0:T(8,128)} %neigh_hbm.1, s32[6,512]{1,0:T(8,128)} %orient_hbm.1, s32[2,256]{1,0:T(2,128)} %list_hbm.1, ...), custom_call_target="tpu_custom_call" | custom-call | tf_op jit(solution)/shard_map/pallas_call | solution.py:570
  24.0 0.9 %fusion = (f32[125,512]{1,0:T(8,128)}, f32[125,512]{1,0:T(8,128)}) fusion(f32[3,128,512]{2,1,0:T(8,128)S(1)} %get-tuple-element.6, f32[512]{0:T(512)S(1)} %bitcast.23, f32[512]{0:T(512)S(1)} %bitcast.22), kind=kLoop, calls=%fused_computation.1 | loop fusion | flops 448000 | bytes 1284096 | tf_op jit(solution)/shard_map/add | solution.py:608

commit v2 on v1

--- a/solution.py
+++ b/solution.py
@@ -155,6 +155,14 @@
     return lax.broadcasted_iota(jnp.int32, shape, dim)
 
 
+def rounds_of(group):
+    rounds, reach = [(1, 2)], 2
+    while reach < group - 1:
+        rounds.append((reach,))
+        reach *= 2
+    return rounds
+
+
 def kernel(
     shape,
     rhs_hbm,
@@ -199,6 +207,7 @@
     halo_recv,
     sum_send,
     sum_recv,
+    seen,
 ):
     curve, group = shape
     ranks = curve * group
@@ -227,9 +236,8 @@
                 for side, device in ((0, other(ranks - reach)), (1, other(reach)))
             ]
 
-        def start(self):
-            for side in range(2):
-                pl.when(self.there[side])(self.copies[side].start)
+        def start(self, side):
+            pl.when(self.there[side])(self.copies[side].start)
 
         def arrive(self, side):
             pl.when(self.there[side])(self.copies[1 - side].wait_recv)
@@ -265,9 +273,34 @@
         else:
             pl.loop(0, group)(one)
 
-    for_each_other(
-        lambda device: pl.semaphore_signal(barrier, inc=1, device_id=device, device_id_type=MESH)
-    )
+    def signal(semaphore, device):
+        pl.semaphore_signal(semaphore, inc=1, device_id=device, device_id_type=MESH)
+
+    greeted = curve - 1
+    for step in (2, 1):
+        for there, device in (
+            (me + step < ranks, other(step)),
+            (me >= step, other(ranks - step)),
+        ):
+            pl.when(there)(functools.partial(signal, barrier, device))
+            greeted = greeted + there.astype(jnp.int32)
+    for step in range(1, curve):
+        signal(barrier, (lax.rem(my_curve + step, curve), my_group))
+
+    def spread(index):
+        for step in rounds_of(group)[index]:
+            for there, to in (
+                (my_group + step < group, my_group + step),
+                (my_group >= step, my_group - step),
+            ):
+                pl.when(there)(functools.partial(signal, seen.at[index], (my_curve, to)))
+
+    def gather(index):
+        count = 0
+        for step in rounds_of(group)[index]:
+            count = count + (my_group + step < group).astype(jnp.int32)
+            count = count + (my_group >= step).astype(jnp.int32)
+        pl.semaphore_wait(seen.at[index], count)
 
     loads = [
         pltpu.make_async_copy(source, target, load_sem.at[index])
@@ -333,10 +366,11 @@
     packed[0] = chosen[:MOVE]
     packed[1] = chosen[MOVE:]
 
-    pl.semaphore_wait(barrier, ranks - 1)
+    pl.semaphore_wait(barrier, greeted)
 
     moves = Exchange(packed, moved, move_send, move_recv, 1)
-    moves.start()
+    for side in range(2):
+        moves.start(side)
 
     for load in loads[4:]:
         load.wait()
@@ -373,8 +407,10 @@
 
     halos = Exchange(halo_out.at[0], halo_in.at[0], halo_send.at[0], halo_recv.at[0], 1)
     fars = Exchange(far_out, far_in, far_send, far_recv, 2)
-    fars.start()
-    halos.start()
+    for copies in (fars, halos):
+        for side in range(2):
+            copies.start(side)
+    spread(0)
 
     stay = one_hot(iota((cells, cells), 0), offset)
     arrived = dot_last(parts, stay)
@@ -462,6 +498,7 @@
     for side in range(2):
         halos.arrive(side)
         fars.arrive(side)
+    gather(0)
     terms = []
     for face in range(2):
         ghosts = widen(halo_in[0, face])
@@ -475,13 +512,18 @@
     image = result + lifted(terms, 0, 2)
 
     stacked = stack(image)
-    own, halves = faces_of(stacked, kappa, 0, 2)
-    for side in range(2):
-        halo_out[1, side] = shrink(dot(halves[side], send_hot[side]))
     images = Exchange(halo_out.at[1], halo_in.at[1], halo_send.at[1], halo_recv.at[1], 1)
-    images.start()
+    own_right, halves_right = faces_of(stacked, kappa, 1, 2)
+    halo_out[1, 1] = shrink(dot(halves_right[0], send_hot[1]))
+    images.start(1)
+    if len(rounds_of(group)) > 1:
+        spread(1)
     basis[1] = image
+    own_left, halves_left = faces_of(stacked, kappa, 0, 1)
+    own, halves = own_left + own_right, halves_left + halves_right
     result, near = inner(image, stacked, halves)
+    halo_out[1, 0] = shrink(dot(halves[0], send_hot[0]))
+    images.start(0)
     value, flux = own[1]
     edge = 2.0 * outer(1) * down(face_weight * (value * (PENALTY * kappa * value - flux)))
     found = [across(down(field * field)), across(down(field * image)), across(down(image * image))]
@@ -508,7 +550,14 @@
     slot_weight = face_weight * bits[2:3]
     slot_kappa = across_edge[FACE_KAPPA : FACE_KAPPA + 1]
 
+    for index in range(1, len(rounds_of(group))):
+        if index > 1:
+            spread(index)
+        if index < len(rounds_of(group)) - 1:
+            gather(index)
     images.arrive(0)
+    if len(rounds_of(group)) > 1:
+        gather(len(rounds_of(group)) - 1)
     ghosts = widen(halo_in[1, 0])
     penalty = PENALTY * jnp.maximum(slot_kappa, ghosts[FACE_KAPPA : FACE_KAPPA + 1])
     jump = across_edge[:PART] - slot_sign * ghosts[:PART]
@@ -599,6 +648,7 @@
             dma((2, 2)),
             dma,
             dma,
+            pltpu.SemaphoreType.REGULAR((len(rounds_of(shape[1])),)),
         ],
         compiler_params=pltpu.CompilerParams(
             collective_id=0, has_side_effects=True, vmem_limit_bytes=VMEM_LIMIT

time: 25 us -> 23.6 us (0.944)
  Pallas kernels: 23.3 us -> 21.9 us
    pallas_call x1, Pallas kernels: 23.3 us -> 21.9 us  [body(): pl.pallas_call(functools.partial(kernel, shape), out_shape=(jax.ShapeDtyp...]
where the time goes in v2:
time: 23.6 us; the launch traced here: 23.5 us
  Pallas kernels  21.9 us (93%)
  other arithmetic  0.88 us (4%)
  between operations  0.64 us (3%)
    pallas_call x1, Pallas kernels, body(): pl.pallas_call(functools.partial(kernel, shape), out_shape=(jax.ShapeDtyp...  21.9 us
    add x1, other arithmetic, body(): first - linear * second + square * third  0.88 us

profile of v2, /device:TPU:0, one launch (start us, length us, event | category | flops | bytes accessed | tf_op | source)
XLA Modules:
  0.0 23.5 jit_solution(13349129663176314717)
XLA Ops:
  0.6 21.9 %shard_map.104 = (f32[3,128,512]{2,1,0:T(8,128)S(1)}, f32[1,512]{1,0:T(1,128)S(1)}, f32[1,512]{1,0:T(1,128)S(1)}) custom-call(f32[125,512]{1,0:T(8,128)} %rhs_hbm.1, f32[1,512]{1,0:T(1,128)} %bitcast.24, s32[1,512]{1,0:T(1,128)} %bitcast.25, s32[6,512]{1,0:T(8,128)} %neigh_hbm.1, s32[6,512]{1,0:T(8,128)} %orient_hbm.1, s32[2,256]{1,0:T(2,128)} %list_hbm.1, ...), custom_call_target="tpu_custom_call" | custom-call | tf_op jit(solution)/shard_map/pallas_call | solution.py:619
  22.6 0.9 %fusion = (f32[125,512]{1,0:T(8,128)}, f32[125,512]{1,0:T(8,128)}) fusion(f32[3,128,512]{2,1,0:T(8,128)S(1)} %get-tuple-element.6, f32[512]{0:T(512)S(1)} %bitcast.23, f32[512]{0:T(512)S(1)} %bitcast.22), kind=kLoop, calls=%fused_computation.1 | loop fusion | flops 448000 | bytes 1284096 | tf_op jit(solution)/shard_map/add | solution.py:658

commit v3 on v2

--- a/solution.py
+++ b/solution.py
@@ -109,15 +109,17 @@
             normals[face % 2][None, :], face // 2
         )
     lift = trace.T.copy()
+    right = trace[FACE : 2 * FACE].copy()
     for face in range(6):
         trace[face * FACE + FACE_KAPPA, KAPPA] = 1.0
-    first = np.zeros((6 * FACE + ROWS, ROWS))
+    first = np.zeros((6 * FACE + 2 * ROWS, ROWS))
     first[: 6 * FACE] = trace
     first[6 * FACE : 6 * FACE + BLOCK, :BLOCK] = stiffness
+    first[6 * FACE + ROWS : 7 * FACE + ROWS, :BLOCK] = right[:, :BLOCK] @ stiffness
+    first[7 * FACE + ROWS :, :BLOCK] = right[:, :BLOCK] * cell_weight
     high, low = split_table(first)
     forward = np.concatenate([high, high, low], 1)
-    high, low = split_table(lift)
-    backward = np.concatenate([high, low], 0)
+    backward = np.concatenate(split_table(lift) + split_table(right @ lift), 0)
     columns = np.zeros((ROWS, ROWS), np.float32)
     columns[:BLOCK, 0] = cell_weight
     columns[:count, 1] = np.kron(row_weight, row_weight)
@@ -198,6 +200,11 @@
     halo_in,
     sums,
     kept,
+    near_ref,
+    tag_out,
+    tag_in,
+    tag_send,
+    tag_recv,
     load_sem,
     move_send,
     move_recv,
@@ -320,7 +327,7 @@
     ]
     for load in loads:
         load.start()
-    clear(1, (moved, halo_in.at[0], halo_in.at[1]))
+    clear(1, (moved, tag_in, halo_in.at[0], halo_in.at[1]))
     clear(2, (far_in,))
     for load in loads[:4]:
         load.wait()
@@ -366,18 +373,23 @@
     packed[0] = chosen[:MOVE]
     packed[1] = chosen[MOVE:]
 
+    lists = list_ref[...].astype(F32)
+    for side in range(2):
+        tag_out[side] = lists[side : side + 1, :]
+
     pl.semaphore_wait(barrier, greeted)
 
     moves = Exchange(packed, moved, move_send, move_recv, 1)
-    for side in range(2):
-        moves.start(side)
+    tags = Exchange(tag_out, tag_in, tag_send, tag_recv, 1)
+    for copies in (moves, tags):
+        for side in range(2):
+            copies.start(side)
 
     for load in loads[4:]:
         load.wait()
 
     old_halves = faces_of(jnp.concatenate([high, mid, high], 0), cond_ref[...], 0, 2)[1]
     offset_column = jnp.broadcast_to(offset.astype(F32), (8, cells)).T[:, 0:1]
-    lists = list_ref[...].astype(F32)
     halo_rows = iota((HALO, ghost), 0)
 
     def shrink(out):
@@ -392,9 +404,7 @@
     for side in range(2):
         hot = one_hot(offset_column, lists[side : side + 1, :])
         out = dot(old_halves[side], hot)
-        halo_out[0, side] = jnp.where(
-            halo_rows == FACE_TAG, lists[side : side + 1, :], shrink(out)
-        )
+        halo_out[0, side] = shrink(out)
     lanes = iota((2 * MOVE, ROWS), 1)
     tagged = jnp.where(lanes == FACE_TAG, chosen[:, TAG : TAG + 1], 0.0)
     leaving_low = dot_last(pick, old_halves[0]) + tagged
@@ -424,13 +434,39 @@
         )
         send_hot[side] = one_hot(list_ref[side : side + 1, :], iota((cells, ghost), 0))
 
+    def folded(value):
+        half = value.shape[0] // 2
+        return value[:half] + value[half:]
+
+    arrived = arrived[:ROWS] + arrived[ROWS : 2 * ROWS] + arrived[2 * ROWS :]
+    high, low = split_two(arrived)
+    stay_halves = faces_of(
+        jnp.concatenate([high, low, high], 0), arrived[KAPPA : KAPPA + 1], 0, 6
+    )[1]
+    for face in range(6):
+        near_ref[face] = folded(dot(stay_halves[face ^ 1], local_hot[face]))
+    payload[...] = arrived
+
     for side in range(2):
         moves.arrive(side)
+        tags.arrive(side)
     record = moved[...].reshape(2 * MOVE, ROWS)
     landing = record[:, TAG : TAG + 1].astype(jnp.int32) - 1
-    record_parts = jnp.concatenate(split_three(record.T), 0)
-    arrived = arrived + dot(record_parts, one_hot(landing, iota((2 * MOVE, cells), 1)))
-    arrived = arrived[:ROWS] + arrived[ROWS : 2 * ROWS] + arrived[2 * ROWS :]
+    record = record.T
+    high, mid, low = split_three(record)
+    placed = dot(
+        jnp.concatenate([high, mid, low], 0), one_hot(landing, iota((2 * MOVE, cells), 1))
+    )
+    arrived = payload[...] + (placed[:ROWS] + placed[ROWS : 2 * ROWS] + placed[2 * ROWS :])
+    moved_halves = faces_of(
+        jnp.concatenate([high, mid, high], 0), record[KAPPA : KAPPA + 1], 0, 6
+    )[1]
+    landing = jnp.where(landing < 0, -2, landing)
+
+    def near_old(face):
+        hot = one_hot(landing, neigh_ref[face : face + 1, :])
+        return near_ref[face] + folded(dot(moved_halves[face ^ 1], hot))
+
     rows = iota((ROWS, cells), 0)
     field = jnp.where(rows < BLOCK, arrived, 0.0)
     kappa = arrived[KAPPA : KAPPA + 1]
@@ -452,7 +488,6 @@
         value, flux = own
         sign = signs(face)
         outside = outer(face)
-        near = near[:FACE] + near[FACE:]
         near_kappa = near[FACE_KAPPA : FACE_KAPPA + 1] + outside * kappa
         penalty = PENALTY * jnp.maximum(kappa, near_kappa)
         jump = value - (sign * near[:PART] - outside * value)
@@ -461,29 +496,36 @@
         first = face_weight * (penalty * jump - 0.5 * mean)
         return (first, kappa * scaled), (jump, mean, first, scaled)
 
-    def lifted(terms, first, last):
-        high, low = split_two(jnp.concatenate(terms, 0))
-        both = dot(backward_ref[:, first * FACE : last * FACE], high)
+    def lifted(parts, first, last):
+        high, low = parts
+        both = dot(backward_ref[0 : 2 * ROWS, first * FACE : last * FACE], high)
         rest = dot(backward_ref[0:ROWS, first * FACE : last * FACE], low)
         return both[:ROWS] + both[ROWS:] + rest
+
+    def traced(parts, first, last):
+        high, low = parts
+        both = dot(backward_ref[2 * ROWS :, first * FACE : last * FACE], high)
+        rest = dot(backward_ref[2 * ROWS : 2 * ROWS + FACE, first * FACE : last * FACE], low)
+        return both[:FACE] + both[FACE:] + rest
+
+    def split_terms(terms):
+        return split_two(jnp.concatenate(terms, 0))
 
     def stack(field):
         high, low = split_two(jnp.where(rows == KAPPA, kappa, field))
         return jnp.concatenate([high, low, high], 0)
 
-    def inner(field, stacked, halves):
-        more_own, more_halves = faces_of(stacked, kappa, 2, 6)
+    def inner(field, stacked, own, near):
         terms = []
         for face in range(2, 6):
-            near = dot(more_halves[(face ^ 1) - 2], local_hot[face])
-            terms += coefficients(face, more_own[face - 2], near)[0]
-        result = lifted(terms, 2, 6)
-        stiff = dot(forward_ref[6 * FACE :, :], stacked)
-        result = result + cell_weight * field + kappa * stiff
-        return result, [dot(halves[face ^ 1], local_hot[face]) for face in range(2)]
+            terms += coefficients(face, own[face], near(face))[0]
+        stiff = dot(forward_ref[6 * FACE : 6 * FACE + ROWS, :], stacked)
+        terms = split_terms(terms)
+        result = lifted(terms, 2, 6) + cell_weight * field + kappa * stiff
+        return result, [near(face) for face in range(2)], terms
 
     def with_ghosts(near, ghosts, side):
-        return near + dot(jnp.concatenate(split_two(ghosts), 0), ghost_hot[side])
+        return near + folded(dot(jnp.concatenate(split_two(ghosts), 0), ghost_hot[side]))
 
     def down(value):
         return jnp.sum(value, 0, keepdims=True)
@@ -493,35 +535,45 @@
 
     basis[0] = field
     stacked = stack(field)
-    own, halves = faces_of(stacked, kappa, 0, 2)
-    result, near = inner(field, stacked, halves)
+    own = faces_of(stacked, kappa, 0, 6)[0]
+    result, near, terms = inner(field, stacked, own, near_old)
+    volume = dot(forward_ref[6 * FACE + ROWS :, :], stacked)
+    trace = traced(terms, 2, 6) + kappa * volume[:FACE] + volume[FACE:]
+    marks = []
+    for side in range(2):
+        mark = jnp.concatenate(split_two(jnp.broadcast_to(tag_in[side] + 1.0, (8, ghost))), 0)
+        mark = dot(mark, ghost_hot[side])
+        mark = mark[0:1] + mark[8:9]
+        marks.append(jnp.where(mark == 0.0, -1.0, mark))
     for side in range(2):
         halos.arrive(side)
         fars.arrive(side)
     gather(0)
     terms = []
     for face in range(2):
-        ghosts = widen(halo_in[0, face])
         gone = leaving_high[:MOVE] if face == 0 else leaving_low[MOVE:]
         far = far_in[face]
         wide = jnp.concatenate([far[:, :FACE], far[:, FACE:], gone], 0)
-        hot = one_hot(wide[:, FACE_TAG : FACE_TAG + 1] - 1.0, ghosts[FACE_TAG : FACE_TAG + 1])
+        hot = one_hot(wide[:, FACE_TAG : FACE_TAG + 1], marks[face])
         placed = dot(jnp.concatenate(split_two(wide.T), 0), hot)
-        ghosts = ghosts + placed[:FACE] + placed[FACE:]
-        terms += coefficients(face, own[face], with_ghosts(near[face], ghosts, face))[0]
-    image = result + lifted(terms, 0, 2)
-
-    stacked = stack(image)
+        ghosts = with_ghosts(near[face], widen(halo_in[0, face]), face) + folded(placed)
+        terms += coefficients(face, own[face], ghosts)[0]
+    terms = split_terms(terms)
+    trace = trace + traced(terms, 0, 2)
+    value = jnp.where(iota((PART, cells), 0) == FACE_KAPPA, kappa, trace[:PART])
+    parts = jnp.concatenate(split_two(jnp.concatenate([value, kappa * trace[PART:]], 0)), 0)
+    halo_out[1, 1] = shrink(dot(parts, send_hot[1]))
     images = Exchange(halo_out.at[1], halo_in.at[1], halo_send.at[1], halo_recv.at[1], 1)
-    own_right, halves_right = faces_of(stacked, kappa, 1, 2)
-    halo_out[1, 1] = shrink(dot(halves_right[0], send_hot[1]))
     images.start(1)
     if len(rounds_of(group)) > 1:
         spread(1)
+    image = result + lifted(terms, 0, 2)
     basis[1] = image
-    own_left, halves_left = faces_of(stacked, kappa, 0, 1)
-    own, halves = own_left + own_right, halves_left + halves_right
-    result, near = inner(image, stacked, halves)
+    stacked = stack(image)
+    own, halves = faces_of(stacked, kappa, 0, 6)
+    result, near, _ = inner(
+        image, stacked, own, lambda face: folded(dot(halves[face ^ 1], local_hot[face]))
+    )
     halo_out[1, 0] = shrink(dot(halves[0], send_hot[0]))
     images.start(0)
     value, flux = own[1]
@@ -581,8 +633,8 @@
     near[0] = kept[...]
     for face in range(2):
         terms += coefficients(face, own[face], with_ghosts(near[face], widen(halo_in[1, face]), face))[0]
-    basis[2] = result + lifted(terms, 0, 2)
-    for copies in (moves, halos, fars, images):
+    basis[2] = result + lifted(split_terms(terms), 0, 2)
+    for copies in (moves, tags, halos, fars, images):
         copies.leave()
     rest = sums.at[pl.ds(1, ranks - 1)]
     pltpu.make_async_copy(rest, rest, sum_send).wait()
@@ -638,7 +690,12 @@
             pltpu.VMEM((2, 2, HALO, ghost), F32),
             pltpu.VMEM((2, 2, HALO, ghost), F32),
             pltpu.VMEM((ranks, 1, ROWS), F32),
-            pltpu.VMEM((2 * FACE, cells), F32),
+            pltpu.VMEM((FACE, cells), F32),
+            pltpu.VMEM((6, FACE, cells), F32),
+            pltpu.VMEM((2, 1, ghost), F32),
+            pltpu.VMEM((2, 1, ghost), F32),
+            dma((2,)),
+            dma((2,)),
             dma((len(operands),)),
             dma((2,)),
             dma((2,)),

time: 23.6 us -> 23.1 us (0.979)
  Pallas kernels: 21.9 us -> 21.4 us
    pallas_call x1, Pallas kernels: 21.9 us -> 21.4 us  [body(): pl.pallas_call(functools.partial(kernel, shape), out_shape=(jax.ShapeDtyp...]
where the time goes in v3:
time: 23.1 us; the launch traced here: 22.9 us
  Pallas kernels  21.4 us (93%)
  other arithmetic  0.88 us (4%)
  between operations  0.64 us (3%)
    pallas_call x1, Pallas kernels, body(): pl.pallas_call(functools.partial(kernel, shape), out_shape=(jax.ShapeDtyp...  21.4 us
    add x1, other arithmetic, body(): first - linear * second + square * third  0.88 us

profile of v3, /device:TPU:0, one launch (start us, length us, event | category | flops | bytes accessed | tf_op | source)
XLA Modules:
  0.0 22.9 jit_solution(6908512461140856663)
XLA Ops:
  0.6 21.4 %shard_map.104 = (f32[3,128,512]{2,1,0:T(8,128)S(1)}, f32[1,512]{1,0:T(1,128)S(1)}, f32[1,512]{1,0:T(1,128)S(1)}) custom-call(f32[125,512]{1,0:T(8,128)} %rhs_hbm.1, f32[1,512]{1,0:T(1,128)} %bitcast.24, s32[1,512]{1,0:T(1,128)} %bitcast.25, s32[6,512]{1,0:T(8,128)} %neigh_hbm.1, s32[6,512]{1,0:T(8,128)} %orient_hbm.1, s32[2,256]{1,0:T(2,128)} %list_hbm.1, ...), custom_call_target="tpu_custom_call" | custom-call | tf_op jit(solution)/shard_map/pallas_call | solution.py:671
  22.0 0.9 %fusion = (f32[125,512]{1,0:T(8,128)}, f32[125,512]{1,0:T(8,128)}) fusion(f32[3,128,512]{2,1,0:T(8,128)S(1)} %get-tuple-element.6, f32[512]{0:T(512)S(1)} %bitcast.23, f32[512]{0:T(512)S(1)} %bitcast.22), kind=kLoop, calls=%fused_computation.1 | loop fusion | flops 448000 | bytes 1284096 | tf_op jit(solution)/shard_map/add | solution.py:715

commit v4 on v3

--- a/solution.py
+++ b/solution.py
@@ -200,6 +200,12 @@
     halo_in,
     sums,
     kept,
+    shared,
+    slot_out,
+    slot_in,
+    edge_in,
+    edge_send,
+    edge_recv,
     near_ref,
     tag_out,
     tag_in,
@@ -283,7 +289,15 @@
     def signal(semaphore, device):
         pl.semaphore_signal(semaphore, inc=1, device_id=device, device_id_type=MESH)
 
-    greeted = curve - 1
+    wide_group = group > 2
+    odd = lax.rem(my_curve, 2) == 1
+    paired = odd & (my_curve + 1 < curve) & wide_group
+    helps = paired & (my_group == 0)
+    reports = paired & (my_group == group - 1)
+    defers = jnp.logical_not(odd) & (my_curve > 0) & (my_group == 0) & wide_group
+    greeted = curve - 1 + helps.astype(jnp.int32) + reports.astype(jnp.int32)
+    pl.when(reports)(functools.partial(signal, barrier, (my_curve, 0)))
+    pl.when(helps)(functools.partial(signal, barrier, (my_curve, group - 1)))
     for step in (2, 1):
         for there, device in (
             (me + step < ranks, other(step)),
@@ -381,9 +395,10 @@
 
     moves = Exchange(packed, moved, move_send, move_recv, 1)
     tags = Exchange(tag_out, tag_in, tag_send, tag_recv, 1)
-    for copies in (moves, tags):
-        for side in range(2):
-            copies.start(side)
+    moves.start(0)
+    pl.when(my_group > 0)(functools.partial(moves.start, 1))
+    for side in range(2):
+        tags.start(side)
 
     for load in loads[4:]:
         load.wait()
@@ -417,9 +432,11 @@
 
     halos = Exchange(halo_out.at[0], halo_in.at[0], halo_send.at[0], halo_recv.at[0], 1)
     fars = Exchange(far_out, far_in, far_send, far_recv, 2)
-    for copies in (fars, halos):
-        for side in range(2):
-            copies.start(side)
+    halos.start(0)
+    pl.when(my_group == 0)(functools.partial(moves.start, 1))
+    for side in range(2):
+        fars.start(side)
+    halos.start(1)
     spread(0)
 
     stay = one_hot(iota((cells, cells), 0), offset)
@@ -564,6 +581,15 @@
     parts = jnp.concatenate(split_two(jnp.concatenate([value, kappa * trace[PART:]], 0)), 0)
     halo_out[1, 1] = shrink(dot(parts, send_hot[1]))
     images = Exchange(halo_out.at[1], halo_in.at[1], halo_send.at[1], halo_recv.at[1], 1)
+    report = pltpu.make_async_remote_copy(
+        src_ref=halo_out.at[1, 1],
+        dst_ref=edge_in,
+        send_sem=edge_send.at[0],
+        recv_sem=edge_recv.at[0],
+        device_id=(my_curve, 0),
+        device_id_type=MESH,
+    )
+    pl.when(reports)(report.start)
     images.start(1)
     if len(rounds_of(group)) > 1:
         spread(1)
@@ -589,7 +615,7 @@
     lane = iota((1, ROWS), 1)
     message = jnp.zeros((1, ROWS), F32)
     for index, value in enumerate(found):
-        message = jnp.where(lane == index, value, message)
+        message = jnp.where(lax.rem(lane, 4) == index, value, message)
     across_edge = dot_last(halves[0], ghost_hot[0])
     across_edge = across_edge[:FACE] + across_edge[FACE:]
     code = orient_ref[0:1, :]
@@ -598,24 +624,51 @@
         bit_rows == 0, lax.rem(code, 2), jnp.where(bit_rows == 1, jnp.where(code >= 2, 1, 0), 1)
     )
     bits = dot_last(bits.astype(F32).astype(BF), ghost_hot[0])
-    slot_sign = (1.0 - first_odd * bits[0:1]) * (1.0 - second_odd * bits[1:2])
-    slot_weight = face_weight * bits[2:3]
-    slot_kappa = across_edge[FACE_KAPPA : FACE_KAPPA + 1]
+    for index in range(3):
+        row = iota((FACE, ghost), 0) == FACE_TAG + index
+        across_edge = jnp.where(row, bits[index : index + 1], across_edge)
+    slot_out[...] = across_edge
+    defer = pltpu.make_async_remote_copy(
+        src_ref=slot_out,
+        dst_ref=slot_in,
+        send_sem=edge_send.at[1],
+        recv_sem=edge_recv.at[1],
+        device_id=(lax.rem(my_curve + curve - 1, curve), my_group),
+        device_id_type=MESH,
+    )
+    pl.when(defers)(defer.start)
+
+    def edge_energy(mine, ghosts):
+        bit = mine[FACE_TAG : FACE_TAG + 3]
+        sign = (1.0 - first_odd * bit[0:1]) * (1.0 - second_odd * bit[1:2])
+        kappas = jnp.maximum(mine[FACE_KAPPA : FACE_KAPPA + 1], ghosts[FACE_KAPPA : FACE_KAPPA + 1])
+        jump = mine[:PART] - sign * ghosts[:PART]
+        mean = mine[PART:] - sign * ghosts[PART:]
+        energy = face_weight * bit[2:3] * (jump * (PENALTY * kappas * jump - mean))
+        return jnp.broadcast_to(across(down(energy)), (1, ROWS))
 
     for index in range(1, len(rounds_of(group))):
         if index > 1:
             spread(index)
         if index < len(rounds_of(group)) - 1:
             gather(index)
-    images.arrive(0)
+    shared[...] = jnp.zeros((1, ROWS), F32)
+
+    @pl.when(jnp.logical_not(defers))
+    def _():
+        images.arrive(0)
+        shared[...] = edge_energy(slot_out[...], widen(halo_in[1, 0]))
+
     if len(rounds_of(group)) > 1:
         gather(len(rounds_of(group)) - 1)
-    ghosts = widen(halo_in[1, 0])
-    penalty = PENALTY * jnp.maximum(slot_kappa, ghosts[FACE_KAPPA : FACE_KAPPA + 1])
-    jump = across_edge[:PART] - slot_sign * ghosts[:PART]
-    mean = across_edge[PART:] - slot_sign * ghosts[PART:]
-    shared = across(down(slot_weight * (jump * (penalty * jump - mean))))
-    sums[me] = message + jnp.where(lane == 3, shared, 0.0)
+
+    @pl.when(helps)
+    def _():
+        defer.wait_recv()
+        report.wait_recv()
+        shared[...] += edge_energy(slot_in[...], widen(edge_in[...]))
+
+    sums[me] = message + jnp.where(lax.rem(lane, 4) == 3, shared[...], 0.0)
 
     for_each_other(
         lambda device: pltpu.make_async_remote_copy(
@@ -628,7 +681,10 @@
         ).start()
     )
 
+    pl.when(defers)(functools.partial(images.arrive, 0))
     images.arrive(1)
+    pl.when(defers)(defer.wait_send)
+    pl.when(reports)(report.wait_send)
     terms = []
     near[0] = kept[...]
     for face in range(2):
@@ -640,13 +696,20 @@
     pltpu.make_async_copy(rest, rest, sum_send).wait()
     pltpu.make_async_copy(rest, rest, sum_recv).wait()
     summed = jnp.sum(sums[...], 0)
-    ratios = pltpu.roll(summed, ROWS - 1, 1) / summed
-    low, mid, high = (ratios[:, index : index + 1] for index in range(3))
+    turns = [summed] + [pltpu.roll(summed, turn, 1) for turn in range(1, 4)]
+    phase = lax.rem(lane, 4)
+    totals = []
+    for index in range(4):
+        total = turns[3]
+        for turn in range(3):
+            total = jnp.where(lax.rem(phase + 4 - turn, 4) == index, turns[turn], total)
+        totals.append(total)
+    low, mid, high = (totals[index + 1] / totals[index] for index in range(3))
     scale = 1.0 / (low * mid * (high - mid))
     linear = mid * (high - low) * scale
     square = (mid - low) * scale
-    linear_ref[...] = jnp.broadcast_to(linear, (1, cells))
-    square_ref[...] = jnp.broadcast_to(square, (1, cells))
+    linear_ref[...] = jnp.concatenate([linear] * (cells // ROWS), 1)
+    square_ref[...] = jnp.concatenate([square] * (cells // ROWS), 1)
 
 
 def body(shape, right_side, conductivity, destination, neighbour, orientation, send_list):
@@ -691,6 +754,12 @@
             pltpu.VMEM((2, 2, HALO, ghost), F32),
             pltpu.VMEM((ranks, 1, ROWS), F32),
             pltpu.VMEM((FACE, cells), F32),
+            pltpu.VMEM((1, ROWS), F32),
+            pltpu.VMEM((FACE, ghost), F32),
+            pltpu.VMEM((FACE, ghost), F32),
+            pltpu.VMEM((HALO, ghost), F32),
+            dma((2,)),
+            dma((2,)),
             pltpu.VMEM((6, FACE, cells), F32),
             pltpu.VMEM((2, 1, ghost), F32),
             pltpu.VMEM((2, 1, ghost), F32),

time: 23.1 us -> 22.7 us (0.983)
  Pallas kernels: 21.4 us -> 21 us
    pallas_call x1, Pallas kernels: 21.4 us -> 21 us  [body(): pl.pallas_call(functools.partial(kernel, shape), out_shape=(jax.ShapeDtyp...]
where the time goes in v4:
time: 22.7 us; the launch traced here: 22.6 us
  Pallas kernels  21 us (93%)
  other arithmetic  0.88 us (4%)
  between operations  0.64 us (3%)
    pallas_call x1, Pallas kernels, body(): pl.pallas_call(functools.partial(kernel, shape), out_shape=(jax.ShapeDtyp...  21 us
    add x1, other arithmetic, body(): first - linear * second + square * third  0.88 us

profile of v4, /device:TPU:0, one launch (start us, length us, event | category | flops | bytes accessed | tf_op | source)
XLA Modules:
  0.0 22.6 jit_solution(17373876092512841230)
XLA Ops:
  0.6 21.0 %shard_map.104 = (f32[3,128,512]{2,1,0:T(8,128)S(1)}, f32[1,512]{1,0:T(1,128)S(1)}, f32[1,512]{1,0:T(1,128)S(1)}) custom-call(f32[125,512]{1,0:T(8,128)} %rhs_hbm.1, f32[1,512]{1,0:T(1,128)} %bitcast.24, s32[1,512]{1,0:T(1,128)} %bitcast.25, s32[6,512]{1,0:T(8,128)} %neigh_hbm.1, s32[6,512]{1,0:T(8,128)} %orient_hbm.1, s32[2,256]{1,0:T(2,128)} %list_hbm.1, ...), custom_call_target="tpu_custom_call" | custom-call | tf_op jit(solution)/shard_map/pallas_call | solution.py:734
  21.7 0.9 %fusion = (f32[125,512]{1,0:T(8,128)}, f32[125,512]{1,0:T(8,128)}) fusion(f32[3,128,512]{2,1,0:T(8,128)S(1)} %get-tuple-element.6, f32[512]{0:T(512)S(1)} %bitcast.23, f32[512]{0:T(512)S(1)} %bitcast.22), kind=kLoop, calls=%fused_computation.1 | loop fusion | flops 448000 | bytes 1284096 | tf_op jit(solution)/shard_map/add | solution.py:784

commit v5 on v4

--- a/solution.py
+++ b/solution.py
@@ -432,18 +432,22 @@
 
     halos = Exchange(halo_out.at[0], halo_in.at[0], halo_send.at[0], halo_recv.at[0], 1)
     fars = Exchange(far_out, far_in, far_send, far_recv, 2)
-    halos.start(0)
+    pl.when(my_group == 0)(functools.partial(halos.start, 0))
+    pl.when(my_group > 0)(functools.partial(halos.start, 1))
     pl.when(my_group == 0)(functools.partial(moves.start, 1))
     for side in range(2):
         fars.start(side)
-    halos.start(1)
-    spread(0)
 
     stay = one_hot(iota((cells, cells), 0), offset)
     arrived = dot_last(parts, stay)
     cell_rows = iota((cells, cells), 0)
     ghost_rows = iota((ghost, cells), 0)
-    for face in range(6):
+    for face in range(3):
+        local_hot[face] = one_hot(neigh_ref[face : face + 1, :], cell_rows)
+    pl.when(my_group == 0)(functools.partial(halos.start, 1))
+    pl.when(my_group > 0)(functools.partial(halos.start, 0))
+    spread(0)
+    for face in range(3, 6):
         local_hot[face] = one_hot(neigh_ref[face : face + 1, :], cell_rows)
     for side in range(2):
         ghost_hot[side] = one_hot(

time: 22.7 us -> 22.6 us (level)
  no operation moved by 1% of the time
where the time goes in v5:
time: 22.6 us; the launch traced here: 22.4 us
  Pallas kernels  20.9 us (92%)
  other arithmetic  0.88 us (4%)
  between operations  0.64 us (3%)
    pallas_call x1, Pallas kernels, body(): pl.pallas_call(functools.partial(kernel, shape), out_shape=(jax.ShapeDtyp...  20.9 us
    add x1, other arithmetic, body(): first - linear * second + square * third  0.88 us

profile of v5, /device:TPU:0, one launch (start us, length us, event | category | flops | bytes accessed | tf_op | source)
XLA Modules:
  0.0 22.4 jit_solution(14428649098302039388)
XLA Ops:
  0.6 20.9 %shard_map.104 = (f32[3,128,512]{2,1,0:T(8,128)S(1)}, f32[1,512]{1,0:T(1,128)S(1)}, f32[1,512]{1,0:T(1,128)S(1)}) custom-call(f32[125,512]{1,0:T(8,128)} %rhs_hbm.1, f32[1,512]{1,0:T(1,128)} %bitcast.24, s32[1,512]{1,0:T(1,128)} %bitcast.25, s32[6,512]{1,0:T(8,128)} %neigh_hbm.1, s32[6,512]{1,0:T(8,128)} %orient_hbm.1, s32[2,256]{1,0:T(2,128)} %list_hbm.1, ...), custom_call_target="tpu_custom_call" | custom-call | tf_op jit(solution)/shard_map/pallas_call | solution.py:738
  21.5 0.9 %fusion = (f32[125,512]{1,0:T(8,128)}, f32[125,512]{1,0:T(8,128)}) fusion(f32[3,128,512]{2,1,0:T(8,128)S(1)} %get-tuple-element.6, f32[512]{0:T(512)S(1)} %bitcast.23, f32[512]{0:T(512)S(1)} %bitcast.22), kind=kLoop, calls=%fused_computation.1 | loop fusion | flops 448000 | bytes 1284096 | tf_op jit(solution)/shard_map/add | solution.py:788
